TPU v7x, 32 devices: a whole 2x2x4 slice. The times are simulated.
32 devices in a mesh: row: 8 (over z, x), col: 4 (over y, core).
Axes of the slice: x: 2, y: 2, z: 4, core: 2. Of those that a mesh axis runs over, the one named last changes fastest.
Arguments:
- gradients: bfloat16 [32, 1024, 5120], P(('row', 'col')), may hold values from -24 to 24
- bucket_lengths: int32 [16], replicated, may hold values from 1 to 128, 1024 in all
- owner_offset: int32 [8], replicated, may hold values from 0 to 3
- clip_rms: float32 [1], replicated, may hold values from 0.15 to 0.4
Outputs:
- clipped_shard: float32 [1024, 5120], P('row', 'col')
- bucket_rms: float32 [16], replicated
Inputs may be any that keep to these rules, and one draw needn't show every extreme that they name: `bucket_lengths`: the buckets cover all 1024 rows; the largest has exactly 128 rows.
All inputs are finite; a program needn't handle non-finite values.
Results may differ from a plain program's by a relative error of at most 0.0003.
Values sent between devices are 32-bit elements; how exact they have to be, the bound alone decides.
A program may use at most 128 MiB of HBM per device.

v0:
```python
import jax
import jax.numpy as jnp
from jax import lax
from jax.sharding import PartitionSpec as P


def turn_block(block, shift):
    return jnp.roll(block, -shift, axis=1)


def shards(gradients, bucket_lengths, owner_offset, clip_rms):
    n_row = lax.axis_size("row")
    n_col = lax.axis_size("col")
    devices = n_row * n_col
    source = gradients[0]
    total_rows, width = source.shape
    width_local = width // n_col
    rows_local = total_rows // n_row
    row_index = lax.axis_index("row")
    blocks = source.reshape(n_row, rows_local, n_col, width_local)
    blocks = jax.vmap(turn_block)(blocks, owner_offset)
    blocks = (
        blocks.transpose(0, 2, 1, 3).reshape(devices * rows_local, width_local).astype(jnp.float32)
    )
    summed = lax.psum_scatter(blocks, ("row", "col"), scatter_dimension=0, tiled=True)
    averaged = summed / devices
    ends = jnp.cumsum(bucket_lengths)
    starts = ends - bucket_lengths
    row_ids = row_index * rows_local + jnp.arange(rows_local, dtype=jnp.int32)
    member = ((row_ids[:, None] >= starts[None, :]) & (row_ids[:, None] < ends[None, :])).astype(
        jnp.float32
    )
    row_squares = jnp.sum(averaged * averaged, axis=1)
    local_squares = jnp.sum(row_squares[:, None] * member, axis=0)
    bucket_squares = lax.psum(local_squares, ("row", "col"))
    overall = jnp.sqrt(jnp.sum(bucket_squares) / (total_rows * width))
    factor = clip_rms[0] / jnp.maximum(overall, clip_rms[0])
    clipped_shard = averaged * factor
    bucket_rms = jnp.sqrt(bucket_squares / (bucket_lengths.astype(jnp.float32) * width))
    return (clipped_shard, bucket_rms)


def solution(mesh):
    in_specs = (P(("row", "col"), None, None), P(), P(), P())
    out_specs = (P("row", "col"), P())
    return jax.shard_map(shards, mesh=mesh, in_specs=in_specs, out_specs=out_specs, check_vma=False)
```

profile of v0, /device:TPU:0, one launch (start us, length us, event | category | flops | bytes accessed | tf_op | source)
XLA Modules:
  0.0 363.9 jit_solution(11172365279284914420)
XLA Ops:
  7.2 0.0 reduce-scatter.2.cloned.1.call-start
  7.2 19.4 %reshape.50 = bf16[8,128,4,1280]{3,2,1,0:T(4,128)(2,1)} reshape(bf16[1,1024,5120]{2,1,0:T(8,128)(2,1)} %param.4) | data formatting | bytes 20971520 | tf_op jit(solution)/shard_map/reshape;squeeze | solution.py:20
  26.6 9.8 %copy.12 = bf16[8,128,4,1280]{3,1,0,2:T(8,128)(2,1)} copy(bf16[8,128,4,1280]{3,2,1,0:T(4,128)(2,1)} %reshape.50) | data formatting | bytes 20971520 | tf_op jit(solution)/shard_map/reshape;squeeze | solution.py:20
  36.4 0.0 copy-start.1
  36.4 17.5 %pad_maximum_fusion = bf16[8,128,8,1280]{3,1,0,2:T(8,128)(2,1)} fusion(bf16[8,128,4,1280]{3,1,0,2:T(8,128)(2,1)} %copy.12), kind=kLoop, calls=%fused_computation.1 | loop fusion | flops 10485760 | bytes 31457280 | tf_op jit(solution)/shard_map/vmap(jit(_roll_dynamic))/concatenate | solution.py:8
  53.9 0.0 copy-done.1
  54.0 12.7 %gather_fusion = bf16[8,128,4,1280]{3,1,2,0:T(8,128)(2,1)} fusion(bf16[8,128,8,1280]{3,1,0,2:T(8,128)(2,1)} %pad_maximum_fusion, s32[8]{0:T(128)S(1)} %fusion.2), kind=kCustom, calls=%fused_computation | custom fusion | bytes 20971648 | tf_op jit(solution)/shard_map/vmap(jit(_roll_dynamic))/gather | solution.py:8
  66.6 13.6 %convert_element_type.18 = f32[8,128,4,1280]{3,1,2,0:T(8,128)} convert(bf16[8,128,4,1280]{3,1,2,0:T(8,128)(2,1)} %gather_fusion) | non-fusion elementwise | flops 5242880 | bytes 31457280 | tf_op jit(solution)/shard_map/convert_element_type | solution.py:23
  80.2 0.0 copy-start
  80.2 0.0 reduce-scatter.2.cloned.1.call-update
  80.3 0.6 copy-done
  80.9 0.1 copy.14
  81.0 0.1 reduce
  81.1 227.2 %reduce-scatter.2.cloned.1.call-done = f32[128,1280]{1,0:T(8,128)} async-done(((f32[4096,1280]{1,0:T(8,128)}), f32[128,1280]{1,0:T(8,128)}) %reduce-scatter.2.cloned.1.call-update) | async-done | bytes 655376 | tf_op jit(solution)/shard_map/reduce_scatter | solution.py:25
  308.3 1.2 multiply_reduce_fusion
  309.6 0.2 select_reduce_fusion
  310.4 42.7 %psum.7 = f32[16]{0:T(128)S(1)} all-reduce(f32[16]{0:T(128)S(1)} %select_reduce_fusion), channel_id=1, replica_groups=mesh['row'=8,'col'=4] {'row','col'}, use_global_device_ids=true, to_apply=%region_4.5 | all-reduce | flops 16 | bytes 128 | tf_op jit(solution)/shard_map/psum | solution.py:35
  353.1 1.2 fusion.3
  355.1 2.0 broadcast_multiply_fusion
  (4 shorter events, 0.1 us)
Async XLA Ops:
  7.2 301.2 %reduce-scatter.2.cloned.1.call-start = ((), (), s32[]{:S(2)}) async-start(), calls=%async_computation.1 | async-start | bytes 21626880 | tf_op jit(solution)/shard_map/reduce_scatter | solution.py:25
  36.4 17.5 %copy-start.1 = (s32[8]{0:T(128)S(1)}, s32[8]{0:T(128)}, u32[]{:S(2)}) copy-start(s32[8]{0:T(128)} %param.6) | copy-start | bytes 100
  80.2 0.7 copy-start
Sparse Core Ops, SparseCore 0:
  80.4 227.9 reduce-scatter.1
where the time goes:
time: 365 us; the launch traced here: 364 us
  waiting for transfers between devices  227 us (62%)
  blocking collectives  42.7 us (12%)
  local copies, waits for them, and re-layouts  42.6 us (12%)
  other arithmetic  35.9 us (10%)
  between operations  15.5 us (4%)
    reduce_scatter x1, waiting for transfers between devices, shards(): lax.psum_scatter(blocks, ('row', 'col'), scatter_dimension=0, tiled=True)  227 us
    psum x1, blocking collectives, shards(): bucket_squares = lax.psum(local_squares, ('row', 'col'))  42.7 us
    another operation x2, local copies, waits for them, and re-layouts, shards(): blocks = source.reshape(n_row, rows_local, n_col, width_local)  29.2 us
    concatenate x1, other arithmetic, turn_block(): return jnp.roll(block, -shift, axis=1)  17.5 us
    convert_element_type x1, other arithmetic, shards(): blocks.transpose(0, 2, 1, 3).reshape(devices * rows_local, width_local)  13.6 us
    gather x1, local copies, waits for them, and re-layouts, turn_block(): return jnp.roll(block, -shift, axis=1)  12.7 us
  transfers between devices with their start and end apart: 1, of which 1 were waited for; matrix products, arithmetic and copies ran while one was open for 0% of the time, Pallas kernels for 0%

commit v1 on v0

--- a/solution.py
+++ b/solution.py
@@ -32,7 +32,7 @@
     )
     row_squares = jnp.sum(averaged * averaged, axis=1)
     local_squares = jnp.sum(row_squares[:, None] * member, axis=0)
-    bucket_squares = lax.psum(local_squares, ("row", "col"))
+    bucket_squares = lax.psum(lax.psum(local_squares, "col"), "row")
     overall = jnp.sqrt(jnp.sum(bucket_squares) / (total_rows * width))
     factor = clip_rms[0] / jnp.maximum(overall, clip_rms[0])
     clipped_shard = averaged * factor

time: 365 us -> 351 us (0.962)
  blocking collectives: 42.7 us -> 29.2 us
    psum x1 -> x2, blocking collectives: 42.7 us -> 29.2 us  [shards(): bucket_squares = lax.psum(lax.psum(local_squares, 'col'), 'row')]
where the time goes in v1:
time: 351 us; the launch traced here: 350 us
  waiting for transfers between devices  227 us (65%)
  local copies, waits for them, and re-layouts  42.6 us (12%)
  other arithmetic  35.9 us (10%)
  blocking collectives  29.2 us (8%)
  between operations  15.5 us (4%)
    reduce_scatter x1, waiting for transfers between devices, shards(): lax.psum_scatter(blocks, ('row', 'col'), scatter_dimension=0, tiled=True)  227 us
    psum x2, blocking collectives, shards(): bucket_squares = lax.psum(lax.psum(local_squares, 'col'), 'row')  29.2 us
    another operation x2, local copies, waits for them, and re-layouts, shards(): blocks = source.reshape(n_row, rows_local, n_col, width_local)  29.2 us
    concatenate x1, other arithmetic, turn_block(): return jnp.roll(block, -shift, axis=1)  17.5 us
    convert_element_type x1, other arithmetic, shards(): blocks.transpose(0, 2, 1, 3).reshape(devices * rows_local, width_local)  13.6 us
    gather x1, local copies, waits for them, and re-layouts, turn_block(): return jnp.roll(block, -shift, axis=1)  12.7 us
  transfers between devices with their start and end apart: 1, of which 1 were waited for; matrix products, arithmetic and copies ran while one was open for 0% of the time, Pallas kernels for 0%

profile of v1, /device:TPU:0, one launch (start us, length us, event | category | flops | bytes accessed | tf_op | source)
XLA Modules:
  0.0 350.4 jit_solution(12839309980723878688)
XLA Ops:
  7.2 0.0 reduce-scatter.2.cloned.1.call-start
  7.2 19.4 %reshape.50 = bf16[8,128,4,1280]{3,2,1,0:T(4,128)(2,1)} reshape(bf16[1,1024,5120]{2,1,0:T(8,128)(2,1)} %param.4) | data formatting | bytes 20971520 | tf_op jit(solution)/shard_map/reshape;squeeze | solution.py:20
  26.6 9.8 %copy.12 = bf16[8,128,4,1280]{3,1,0,2:T(8,128)(2,1)} copy(bf16[8,128,4,1280]{3,2,1,0:T(4,128)(2,1)} %reshape.50) | data formatting | bytes 20971520 | tf_op jit(solution)/shard_map/reshape;squeeze | solution.py:20
  36.4 0.0 copy-start.1
  36.4 17.5 %pad_maximum_fusion = bf16[8,128,8,1280]{3,1,0,2:T(8,128)(2,1)} fusion(bf16[8,128,4,1280]{3,1,0,2:T(8,128)(2,1)} %copy.12), kind=kLoop, calls=%fused_computation.1 | loop fusion | flops 10485760 | bytes 31457280 | tf_op jit(solution)/shard_map/vmap(jit(_roll_dynamic))/concatenate | solution.py:8
  53.9 0.0 copy-done.1
  54.0 12.7 %gather_fusion = bf16[8,128,4,1280]{3,1,2,0:T(8,128)(2,1)} fusion(bf16[8,128,8,1280]{3,1,0,2:T(8,128)(2,1)} %pad_maximum_fusion, s32[8]{0:T(128)S(1)} %fusion.2), kind=kCustom, calls=%fused_computation | custom fusion | bytes 20971648 | tf_op jit(solution)/shard_map/vmap(jit(_roll_dynamic))/gather | solution.py:8
  66.6 13.6 %convert_element_type.18 = f32[8,128,4,1280]{3,1,2,0:T(8,128)} convert(bf16[8,128,4,1280]{3,1,2,0:T(8,128)(2,1)} %gather_fusion) | non-fusion elementwise | flops 5242880 | bytes 31457280 | tf_op jit(solution)/shard_map/convert_element_type | solution.py:23
  80.2 0.0 copy-start
  80.2 0.0 reduce-scatter.2.cloned.1.call-update
  80.3 0.6 copy-done
  80.9 0.1 copy.14
  81.0 0.1 reduce
  81.1 227.2 %reduce-scatter.2.cloned.1.call-done = f32[128,1280]{1,0:T(8,128)} async-done(((f32[4096,1280]{1,0:T(8,128)}), f32[128,1280]{1,0:T(8,128)}) %reduce-scatter.2.cloned.1.call-update) | async-done | bytes 655376 | tf_op jit(solution)/shard_map/reduce_scatter | solution.py:25
  308.3 1.2 multiply_reduce_fusion
  309.6 0.2 select_reduce_fusion
  309.7 8.1 %psum.14 = f32[16]{0:T(128)S(1)} all-reduce(f32[16]{0:T(128)S(1)} %select_reduce_fusion), channel_id=1, replica_groups=mesh['row'=8,'col'=4] {'col'}, use_global_device_ids=true, to_apply=%region_4.5 | all-reduce | flops 16 | bytes 128 | tf_op jit(solution)/shard_map/psum | solution.py:35
  318.5 21.1 %psum.15 = f32[16]{0:T(128)S(1)} all-reduce(f32[16]{0:T(128)S(1)} %psum.14), channel_id=1, replica_groups=mesh['row'=8,'col'=4] {'row'}, use_global_device_ids=true, to_apply=%region_5.6 | all-reduce | flops 16 | bytes 128 | tf_op jit(solution)/shard_map/psum | solution.py:35
  339.6 1.2 fusion.3
  341.6 2.0 broadcast_multiply_fusion
  (4 shorter events, 0.1 us)
Async XLA Ops:
  7.2 301.2 %reduce-scatter.2.cloned.1.call-start = ((), (), s32[]{:S(2)}) async-start(), calls=%async_computation.1 | async-start | bytes 21626880 | tf_op jit(solution)/shard_map/reduce_scatter | solution.py:25
  36.4 17.5 %copy-start.1 = (s32[8]{0:T(128)S(1)}, s32[8]{0:T(128)}, u32[]{:S(2)}) copy-start(s32[8]{0:T(128)} %param.6) | copy-start | bytes 100
  80.2 0.7 copy-start
Sparse Core Ops, SparseCore 0:
  80.4 227.9 reduce-scatter.1
